TPU v7x, 32 devices: a whole 2x2x4 slice. The times are simulated.
32 devices in a mesh: seq: 8 (over y, x, core), head: 4 (over z).
Axes of the slice: x: 2, y: 2, z: 4, core: 2. Of those that a mesh axis runs over, the one named last changes fastest.
Arguments:
- queries: bfloat16 [4096, 4096], P('seq', 'head'), may hold values from -72 to 72
- key_heads: bfloat16 [4096, 4096], P('seq', 'head'), may hold values from -6 to 6
- value_heads: bfloat16 [4096, 4096], P('seq', 'head'), may hold values from -6 to 6
- dilation: int32 [4], replicated, may hold values from 1 to 8, as said below
- window: int32 [4], replicated, may hold values from 96 to 192, as said below
Outputs:
- attended: bfloat16 [4096, 4096], P('seq', 'head')
Inputs may be any that keep to these rules, and one draw needn't show every extreme that they name: dilation holds the four numbers 1, 2, 4, 8, each once. Each window lies between 96 and 192; the group whose dilation is 8 has exactly 192.
All inputs are finite; a program needn't handle non-finite values.
Results may differ from a plain program's by a relative error of at most 0.0043.
Values may be sent and summed in bfloat16 or wider, within the bound.
A program may use at most 64 MiB of HBM per device.

v0:
```python
import functools
import math

import jax
import jax.numpy as jnp
from jax import lax
from jax.experimental import pallas as pl
from jax.experimental.pallas import tpu as pltpu
from jax.sharding import PartitionSpec as P

HS = 128
WIN = 192
MOST = 8
BACK = 3
masked_fill = -1e30
MESH = pl.DeviceIdType.MESH


def kernel(
    n,
    chunks,
    dil_ref,
    win_ref,
    q_ref,
    k_ref,
    v_ref,
    o_ref,
    slots,
    own,
    qv,
    ov,
    perm,
    perm_t,
    kvp,
    qp,
    op,
    send_sem,
    recv_sem,
    local_sem,
    out_sem,
):
    length, width = q_ref.shape
    cw = width // chunks
    tile = length // MOST
    behind = -(-WIN // tile)
    me = lax.axis_index("seq")
    core = me % 2
    chip = me // 2
    chips = n // 2
    partner = me + 1 - 2 * core
    wide = math.isqrt(chips)

    def wraps(c):
        return (c % wide == wide - 1) & (c + 2 < chips)

    detour_source = (core == 1) & wraps(chip)
    detour_via = (core == 0) & (chip >= 2) & ((chip - 2) % wide == wide - 1)

    barrier = pltpu.get_barrier_semaphore()
    near = [(step, (me + step >= 0) & (me + step < n)) for step in (-3, -2, -1, 1, 2, 3)]
    for step, there in near:

        @pl.when(there)
        def _():
            pl.semaphore_signal(barrier, inc=1, device_id={"seq": me + step}, device_id_type=MESH)

    pl.semaphore_wait(barrier, jnp.minimum(me, BACK) + jnp.minimum(n - 1 - me, BACK))

    def columns(j):
        return pl.ds(pl.multiple_of(j * cw, cw), cw)

    def place(slot, j, part):
        return slots.at[slot, j, :, pl.ds(part * cw, cw)]

    def remote(kind, src, slot, target, j, part):
        return pltpu.make_async_remote_copy(
            src_ref=src,
            dst_ref=place(slot, j, part),
            send_sem=send_sem.at[kind, j, part],
            recv_sem=recv_sem.at[slot, j, part],
            device_id={"seq": target},
            device_id_type=MESH,
        )

    def mine(kind, slot, step, j, part):
        src = (k_ref, v_ref)[part].at[:, columns(j)]
        return remote(kind, src, slot, me + step, j, part)

    def forward(j, part, which):
        slot = (2, 0)[which]
        return remote(3, place(1, j, part), slot, partner, j, part)

    def detour(j, part):
        return remote(4, place(2, j, part), 1, me - 1, j, part)

    def arrive(slot, j):
        for part in range(2):
            remote(0, place(slot, j, part), slot, partner, j, part).wait_recv()

    outgoing = [
        (1, 1, 2, (me + 2 < n) & jnp.logical_not(detour_source)),
        (2, 2, 3, (core == 1) & (me + 3 < n)),
        (0, 0, 1, core == 0),
    ]

    def local(j):
        return [
            pltpu.make_async_copy(q_ref.at[:, columns(j)], qv.at[j], local_sem.at[0, j]),
            pltpu.make_async_copy(
                k_ref.at[:, columns(j)], own.at[j, :, pl.ds(0, cw)], local_sem.at[1, j]
            ),
            pltpu.make_async_copy(
                v_ref.at[:, columns(j)], own.at[j, :, pl.ds(cw, cw)], local_sem.at[2, j]
            ),
        ]

    def result(j):
        return pltpu.make_async_copy(ov.at[j], o_ref.at[:, columns(j)], out_sem.at[j])

    def begin(j, carry):
        for kind, slot, step, there in outgoing:

            @pl.when(there)
            def _():
                for part in range(2):
                    mine(kind, slot, step, j, part).start()

        for copy in local(j):
            copy.start()
        return carry

    lax.fori_loop(0, chunks, begin, 0)

    for slot in range(BACK):

        @pl.when(me < slot + 1)
        def _():
            slots[slot] = jnp.zeros(slots.shape[1:], slots.dtype)

    group = lax.axis_index("head")
    dilation = dil_ref[group]
    reach = win_ref[group]
    level = (
        (dilation > 1).astype(jnp.int32)
        + (dilation > 2).astype(jnp.int32)
        + (dilation > 4).astype(jnp.int32)
    )
    per_class = length >> level
    row = lax.broadcasted_iota(jnp.int32, (length, length), 0)
    col = lax.broadcasted_iota(jnp.int32, (length, length), 1)

    def target_of(token):
        return (token & (dilation - 1)) * per_class + (token >> level)

    perm[...] = jnp.where(row == target_of(col), 1.0, 0.0).astype(jnp.bfloat16)
    perm_t[...] = jnp.where(col == target_of(row), 1.0, 0.0).astype(jnp.bfloat16)

    span = (behind + 1) * tile
    apart = (
        lax.broadcasted_iota(jnp.int32, (tile, span), 0)
        - lax.broadcasted_iota(jnp.int32, (tile, span), 1)
        + behind * tile
    )
    key_at = lax.broadcasted_iota(jnp.int32, (tile, span), 1)
    inside = (apart >= 0) & (apart < reach)
    scale = HS ** (-0.5)

    def by_level(four):
        pick = jnp.where(dilation > 1, four[1], four[0])
        pick = jnp.where(dilation > 2, four[2], pick)
        return jnp.where(dilation > 4, four[3], pick)

    tiles_here = by_level([MOST, MOST // 2, MOST // 4, MOST // 8])

    def sort_rows(x):
        return jnp.dot(perm[...], x, preferred_element_type=jnp.float32).astype(jnp.bfloat16)

    def fetch(j):
        @pl.when((core == 0) & (chip >= 2))
        def _():
            arrive(2, j)

        @pl.when(detour_via)
        def _():
            for part in range(2):
                detour(j, part).start()

        @pl.when(chip >= 1)
        def _():
            arrive(1, j)

        for which in range(2):

            @pl.when((chip >= 1) & (core == which))
            def _():
                for part in range(2):
                    forward(j, part, which).start()

    def compute(j):
        @pl.when((core == 1) | (chip >= 1))
        def _():
            arrive(0, j)

        @pl.when((core == 1) & (chip >= 1))
        def _():
            arrive(2, j)

        for copy in local(j):
            copy.wait()
        qp[...] = sort_rows(qv[j]).reshape(qp.shape)
        kvp[pl.ds(0, MOST)] = sort_rows(own[j]).reshape(MOST, tile, 2 * cw)
        for slot in range(BACK):
            kvp[pl.ds((slot + 1) * MOST, MOST)] = sort_rows(slots[slot, j]).reshape(
                MOST, tile, 2 * cw
            )
        for t in range(MOST):
            spots = []
            for offset in range(behind + 1):
                found = []
                for held in (MOST, MOST // 2, MOST // 4, MOST // 8):
                    back, at = divmod(t % held - behind + offset, held)
                    found.append(-back * MOST + t // held * held + at)
                spots.append(by_level(found))
            first = by_level([t % held for held in (MOST, MOST // 2, MOST // 4, MOST // 8)])
            valid = inside & (key_at >= tile * (behind - me * tiles_here - first))
            keys_values = jnp.concatenate([kvp[spot] for spot in spots], axis=0)
            for h in range(cw // HS):
                lanes = slice(h * HS, (h + 1) * HS)
                keys = keys_values[:, lanes]
                values = keys_values[:, cw + h * HS : cw + (h + 1) * HS]
                scores = (
                    lax.dot_general(
                        qp[t, :, lanes],
                        keys,
                        (((1,), (1,)), ((), ())),
                        preferred_element_type=jnp.float32,
                    )
                    * scale
                )
                masked = jnp.where(valid, scores, masked_fill)
                peak = jnp.max(masked, axis=-1, keepdims=True)
                weights = jnp.where(valid, jnp.exp(masked - peak), 0.0)
                total = jnp.sum(weights, axis=-1, keepdims=True)
                mixed = jnp.dot(
                    weights.astype(jnp.bfloat16), values, preferred_element_type=jnp.float32
                )
                op[pl.ds(t * tile, tile), lanes] = (mixed / total).astype(jnp.bfloat16)
        ov[j] = jnp.dot(perm_t[...], op[...], preferred_element_type=jnp.float32).astype(
            jnp.bfloat16
        )
        result(j).start()

    def turn(j, carry):
        @pl.when(j < chunks)
        def _():
            fetch(j)

        @pl.when(j >= 1)
        def _():
            compute(j - 1)

        return carry

    lax.fori_loop(0, chunks + 1, turn, 0)

    def finish(j, carry):
        for part in range(2):
            for kind, slot, step, there in outgoing:

                @pl.when(there)
                def _():
                    mine(kind, slot, step, j, part).wait_send()

            @pl.when(chip >= 1)
            def _():
                forward(j, part, 0).wait_send()

            @pl.when(detour_via)
            def _():
                detour(j, part).wait_send()

        result(j).wait()
        return carry

    lax.fori_loop(0, chunks, finish, 0)


def solution(mesh):
    n = mesh.shape["seq"]

    def body(queries, key_heads, value_heads, dilation, window):
        length, width = queries.shape
        chunks = width // HS
        cw = width // chunks
        tile = length // MOST
        half = jnp.bfloat16
        anywhere = pl.BlockSpec(memory_space=pl.ANY)
        scalars = pl.BlockSpec(memory_space=pltpu.SMEM)
        return pl.pallas_call(
            functools.partial(kernel, n, chunks),
            out_shape=jax.ShapeDtypeStruct((length, width), half),
            in_specs=[scalars, scalars, anywhere, anywhere, anywhere],
            out_specs=anywhere,
            scratch_shapes=[
                pltpu.VMEM((BACK, chunks, length, 2 * cw), half),
                pltpu.VMEM((chunks, length, 2 * cw), half),
                pltpu.VMEM((chunks, length, cw), half),
                pltpu.VMEM((chunks, length, cw), half),
                pltpu.VMEM((length, length), half),
                pltpu.VMEM((length, length), half),
                pltpu.VMEM(((BACK + 1) * MOST, tile, 2 * cw), half),
                pltpu.VMEM((MOST, tile, cw), half),
                pltpu.VMEM((length, cw), half),
                pltpu.SemaphoreType.DMA((5, chunks, 2)),
                pltpu.SemaphoreType.DMA((BACK, chunks, 2)),
                pltpu.SemaphoreType.DMA((3, chunks)),
                pltpu.SemaphoreType.DMA((chunks,)),
            ],
            compiler_params=pltpu.CompilerParams(collective_id=0, has_side_effects=True),
        )(dilation, window, queries, key_heads, value_heads)

    return jax.shard_map(
        body,
        mesh=mesh,
        in_specs=(P("seq", "head"), P("seq", "head"), P("seq", "head"), P(), P()),
        out_specs=P("seq", "head"),
        check_vma=False,
    )
```

profile of v0, /device:TPU:21, one launch (start us, length us, event | category | flops | bytes accessed | tf_op | source)
XLA Modules:
  0.0 63.5 jit_solution(9957682963390521639)
XLA Ops:
  0.0 61.2 %shard_map.55 = bf16[512,1024]{1,0:T(8,128)(2,1)} custom-call(s32[4]{0:T(128)} %dil_ref.1, s32[4]{0:T(128)} %win_ref.1, bf16[512,1024]{1,0:T(8,128)(2,1)} %q_ref.1, bf16[512,1024]{1,0:T(8,128)(2,1)} %k_ref.1, bf16[512,1024]{1,0:T(8,128)(2,1)} %v_ref.1), custom_call_target="tpu_custom_call" | custom-call | tf_op jit(solution)/shard_map/pallas_call | solution.py:299
  61.2 2.3 %copy.7 = bf16[512,1024]{1,0:T(8,128)(2,1)} copy(bf16[512,1024]{1,0:T(8,128)(2,1)} %shard_map.55) | data formatting | bytes 2097152
where the time goes:
time: 63.6 us; the launch traced here: 63.5 us
  Pallas kernels  61.2 us (96%)
  local copies, waits for them, and re-layouts  2.26 us (4%)
    pallas_call x1, Pallas kernels, body(): pl.pallas_call(functools.partial(kernel, n, chunks), out_shape=jax.ShapeD...  61.2 us
    unnamed x1, local copies, waits for them, and re-layouts  2.26 us

commit v1 on v0

--- a/solution.py
+++ b/solution.py
@@ -27,12 +27,13 @@
     o_ref,
     slots,
     own,
-    qv,
     ov,
     perm,
     perm_t,
-    kvp,
-    qp,
+    sorted_rows,
+    raw,
+    rounded,
+    totals,
     op,
     send_sem,
     recv_sem,
@@ -70,7 +71,7 @@
         return pl.ds(pl.multiple_of(j * cw, cw), cw)
 
     def place(slot, j, part):
-        return slots.at[slot, j, :, pl.ds(part * cw, cw)]
+        return slots.at[slot, part, j]
 
     def remote(kind, src, slot, target, j, part):
         return pltpu.make_async_remote_copy(
@@ -93,9 +94,8 @@
     def detour(j, part):
         return remote(4, place(2, j, part), 1, me - 1, j, part)
 
-    def arrive(slot, j):
-        for part in range(2):
-            remote(0, place(slot, j, part), slot, partner, j, part).wait_recv()
+    def arrive(slot, j, part):
+        remote(0, place(slot, j, part), slot, partner, j, part).wait_recv()
 
     outgoing = [
         (1, 1, 2, (me + 2 < n) & jnp.logical_not(detour_source)),
@@ -103,16 +103,9 @@
         (0, 0, 1, core == 0),
     ]
 
-    def local(j):
-        return [
-            pltpu.make_async_copy(q_ref.at[:, columns(j)], qv.at[j], local_sem.at[0, j]),
-            pltpu.make_async_copy(
-                k_ref.at[:, columns(j)], own.at[j, :, pl.ds(0, cw)], local_sem.at[1, j]
-            ),
-            pltpu.make_async_copy(
-                v_ref.at[:, columns(j)], own.at[j, :, pl.ds(cw, cw)], local_sem.at[2, j]
-            ),
-        ]
+    def local(part, j):
+        src = (k_ref, v_ref, q_ref)[part].at[:, columns(j)]
+        return pltpu.make_async_copy(src, own.at[part, j], local_sem.at[part, j])
 
     def result(j):
         return pltpu.make_async_copy(ov.at[j], o_ref.at[:, columns(j)], out_sem.at[j])
@@ -125,8 +118,8 @@
                 for part in range(2):
                     mine(kind, slot, step, j, part).start()
 
-        for copy in local(j):
-            copy.start()
+        for part in range(3):
+            local(part, j).start()
         return carry
 
     lax.fori_loop(0, chunks, begin, 0)
@@ -172,96 +165,124 @@
 
     tiles_here = by_level([MOST, MOST // 2, MOST // 4, MOST // 8])
 
-    def sort_rows(x):
-        return jnp.dot(perm[...], x, preferred_element_type=jnp.float32).astype(jnp.bfloat16)
-
-    def fetch(j):
-        @pl.when((core == 0) & (chip >= 2))
-        def _():
-            arrive(2, j)
-
+    def sort_rows(parts):
+        joined = jnp.concatenate(parts, axis=1)
+        moved = jnp.dot(perm[...], joined, preferred_element_type=jnp.float32)
+        moved = moved.astype(jnp.bfloat16).reshape(MOST, tile, joined.shape[1])
+        width_of = parts[0].shape[1]
+        return [moved[:, :, i * width_of : (i + 1) * width_of] for i in range(len(parts))]
+
+    def relay(j):
         @pl.when(detour_via)
         def _():
             for part in range(2):
+                arrive(2, j, part)
                 detour(j, part).start()
 
+    def fetch(j, part):
         @pl.when(chip >= 1)
         def _():
-            arrive(1, j)
+            arrive(1, j, part)
 
         for which in range(2):
 
             @pl.when((chip >= 1) & (core == which))
             def _():
-                for part in range(2):
-                    forward(j, part, which).start()
-
-    def compute(j):
+                forward(j, part, which).start()
+
+        local(part, j).wait()
+        near_rows, far_rows = sort_rows([own[part, j], slots[1, part, j]])
+        sorted_rows[part, pl.ds(0, MOST)] = near_rows
+        sorted_rows[part, pl.ds(2 * MOST, MOST)] = far_rows
+
+    def complete(j, part):
         @pl.when((core == 1) | (chip >= 1))
         def _():
-            arrive(0, j)
-
-        @pl.when((core == 1) & (chip >= 1))
-        def _():
-            arrive(2, j)
-
-        for copy in local(j):
-            copy.wait()
-        qp[...] = sort_rows(qv[j]).reshape(qp.shape)
-        kvp[pl.ds(0, MOST)] = sort_rows(own[j]).reshape(MOST, tile, 2 * cw)
-        for slot in range(BACK):
-            kvp[pl.ds((slot + 1) * MOST, MOST)] = sort_rows(slots[slot, j]).reshape(
-                MOST, tile, 2 * cw
-            )
+            arrive(0, j, part)
+
+        @pl.when(((core == 0) & (chip >= 2) & jnp.logical_not(detour_via)) | ((core == 1) & (chip >= 1)))
+        def _():
+            arrive(2, j, part)
+
+        near_rows, far_rows = sort_rows([slots[0, part, j], slots[2, part, j]])
+        sorted_rows[part, pl.ds(MOST, MOST)] = near_rows
+        sorted_rows[part, pl.ds(3 * MOST, MOST)] = far_rows
+
+    levels_of = (MOST, MOST // 2, MOST // 4, MOST // 8)
+    spots = []
+    firsts = []
+    for t in range(MOST):
+        row_of = []
+        for offset in range(behind + 1):
+            found = []
+            for held in levels_of:
+                back, at = divmod(t % held - behind + offset, held)
+                found.append(-back * MOST + t // held * held + at)
+            row_of.append(by_level(found))
+        spots.append(row_of)
+        firsts.append(by_level([t % held for held in levels_of]))
+
+    def rows_for(part, t):
+        return jnp.concatenate([sorted_rows[part, spot] for spot in spots[t]], axis=0)
+
+    heads = cw // HS
+
+    def score(j):
+        local(2, j).wait()
+        (asked,) = sort_rows([own[2, j]])
+        complete(j, 0)
         for t in range(MOST):
-            spots = []
-            for offset in range(behind + 1):
-                found = []
-                for held in (MOST, MOST // 2, MOST // 4, MOST // 8):
-                    back, at = divmod(t % held - behind + offset, held)
-                    found.append(-back * MOST + t // held * held + at)
-                spots.append(by_level(found))
-            first = by_level([t % held for held in (MOST, MOST // 2, MOST // 4, MOST // 8)])
-            valid = inside & (key_at >= tile * (behind - me * tiles_here - first))
-            keys_values = jnp.concatenate([kvp[spot] for spot in spots], axis=0)
-            for h in range(cw // HS):
+            keys = rows_for(0, t)
+            for h in range(heads):
                 lanes = slice(h * HS, (h + 1) * HS)
-                keys = keys_values[:, lanes]
-                values = keys_values[:, cw + h * HS : cw + (h + 1) * HS]
-                scores = (
-                    lax.dot_general(
-                        qp[t, :, lanes],
-                        keys,
-                        (((1,), (1,)), ((), ())),
-                        preferred_element_type=jnp.float32,
-                    )
-                    * scale
+                raw[h, t] = lax.dot_general(
+                    asked[t, :, lanes],
+                    keys[:, lanes],
+                    (((1,), (1,)), ((), ())),
+                    preferred_element_type=jnp.float32,
                 )
-                masked = jnp.where(valid, scores, masked_fill)
-                peak = jnp.max(masked, axis=-1, keepdims=True)
-                weights = jnp.where(valid, jnp.exp(masked - peak), 0.0)
-                total = jnp.sum(weights, axis=-1, keepdims=True)
+        for t in range(MOST):
+            valid = inside & (key_at >= tile * (behind - me * tiles_here - firsts[t]))
+            for h in range(heads):
+                masked = jnp.where(valid, raw[h, t] * scale, masked_fill)
+                weights = jnp.exp(masked - jnp.max(masked, axis=-1, keepdims=True))
+                totals[h, t] = jnp.sum(weights, axis=-1, keepdims=True)
+                rounded[h, t] = weights.astype(jnp.bfloat16)
+
+    def mix(j):
+        complete(j, 1)
+        for t in range(MOST):
+            values = rows_for(1, t)
+            for h in range(heads):
+                lanes = slice(h * HS, (h + 1) * HS)
                 mixed = jnp.dot(
-                    weights.astype(jnp.bfloat16), values, preferred_element_type=jnp.float32
+                    rounded[h, t], values[:, lanes], preferred_element_type=jnp.float32
                 )
-                op[pl.ds(t * tile, tile), lanes] = (mixed / total).astype(jnp.bfloat16)
+                op[pl.ds(t * tile, tile), lanes] = (mixed / totals[h, t]).astype(jnp.bfloat16)
         ov[j] = jnp.dot(perm_t[...], op[...], preferred_element_type=jnp.float32).astype(
             jnp.bfloat16
         )
         result(j).start()
 
+    relay(0)
+
     def turn(j, carry):
-        @pl.when(j < chunks)
-        def _():
-            fetch(j)
+        @pl.when(j < chunks - 1)
+        def _():
+            relay(j + 1)
+
+        fetch(j, 0)
 
         @pl.when(j >= 1)
         def _():
-            compute(j - 1)
-
+            mix(j - 1)
+
+        score(j)
+        fetch(j, 1)
         return carry
 
-    lax.fori_loop(0, chunks + 1, turn, 0)
+    lax.fori_loop(0, chunks, turn, 0)
+    mix(chunks - 1)
 
     def finish(j, carry):
         for part in range(2):
@@ -293,6 +314,7 @@
         chunks = width // HS
         cw = width // chunks
         tile = length // MOST
+        span = (-(-WIN // tile) + 1) * tile
         half = jnp.bfloat16
         anywhere = pl.BlockSpec(memory_space=pl.ANY)
         scalars = pl.BlockSpec(memory_space=pltpu.SMEM)
@@ -302,14 +324,15 @@
             in_specs=[scalars, scalars, anywhere, anywhere, anywhere],
             out_specs=anywhere,
             scratch_shapes=[
-                pltpu.VMEM((BACK, chunks, length, 2 * cw), half),
-                pltpu.VMEM((chunks, length, 2 * cw), half),
-                pltpu.VMEM((chunks, length, cw), half),
+                pltpu.VMEM((BACK, 2, chunks, length, cw), half),
+                pltpu.VMEM((3, chunks, length, cw), half),
                 pltpu.VMEM((chunks, length, cw), half),
                 pltpu.VMEM((length, length), half),
                 pltpu.VMEM((length, length), half),
-                pltpu.VMEM(((BACK + 1) * MOST, tile, 2 * cw), half),
-                pltpu.VMEM((MOST, tile, cw), half),
+                pltpu.VMEM((2, (BACK + 1) * MOST, tile, cw), half),
+                pltpu.VMEM((cw // HS, MOST, tile, span), jnp.float32),
+                pltpu.VMEM((cw // HS, MOST, tile, span), half),
+                pltpu.VMEM((cw // HS, MOST, tile, 1), jnp.float32),
                 pltpu.VMEM((length, cw), half),
                 pltpu.SemaphoreType.DMA((5, chunks, 2)),
                 pltpu.SemaphoreType.DMA((BACK, chunks, 2)),

time: 63.6 us -> 58.2 us (0.915)
  Pallas kernels: 61.2 us -> 55.7 us
    pallas_call x1, Pallas kernels: 61.2 us -> 55.7 us  [body(): pl.pallas_call(functools.partial(kernel, n, chunks), out_shape=jax.ShapeD...]
where the time goes in v1:
time: 58.2 us; the launch traced here: 58 us
  Pallas kernels  55.7 us (96%)
  local copies, waits for them, and re-layouts  2.26 us (4%)
    pallas_call x1, Pallas kernels, body(): pl.pallas_call(functools.partial(kernel, n, chunks), out_shape=jax.ShapeD...  55.7 us
    unnamed x1, local copies, waits for them, and re-layouts  2.26 us

profile of v1, /device:TPU:21, one launch (start us, length us, event | category | flops | bytes accessed | tf_op | source)
XLA Modules:
  0.0 58.0 jit_solution(9757839621734836384)
XLA Ops:
  0.0 55.7 %shard_map.55 = bf16[512,1024]{1,0:T(8,128)(2,1)} custom-call(s32[4]{0:T(128)} %dil_ref.1, s32[4]{0:T(128)} %win_ref.1, bf16[512,1024]{1,0:T(8,128)(2,1)} %q_ref.1, bf16[512,1024]{1,0:T(8,128)(2,1)} %k_ref.1, bf16[512,1024]{1,0:T(8,128)(2,1)} %v_ref.1), custom_call_target="tpu_custom_call" | custom-call | tf_op jit(solution)/shard_map/pallas_call | solution.py:321
  55.7 2.3 %copy.7 = bf16[512,1024]{1,0:T(8,128)(2,1)} copy(bf16[512,1024]{1,0:T(8,128)(2,1)} %shard_map.55) | data formatting | bytes 2097152

commit v2 on v1

--- a/solution.py
+++ b/solution.py
@@ -27,7 +27,6 @@
     o_ref,
     slots,
     own,
-    ov,
     perm,
     perm_t,
     sorted_rows,
@@ -38,7 +37,6 @@
     send_sem,
     recv_sem,
     local_sem,
-    out_sem,
 ):
     length, width = q_ref.shape
     cw = width // chunks
@@ -106,9 +104,6 @@
     def local(part, j):
         src = (k_ref, v_ref, q_ref)[part].at[:, columns(j)]
         return pltpu.make_async_copy(src, own.at[part, j], local_sem.at[part, j])
-
-    def result(j):
-        return pltpu.make_async_copy(ov.at[j], o_ref.at[:, columns(j)], out_sem.at[j])
 
     def begin(j, carry):
         for kind, slot, step, there in outgoing:
@@ -259,10 +254,9 @@
                     rounded[h, t], values[:, lanes], preferred_element_type=jnp.float32
                 )
                 op[pl.ds(t * tile, tile), lanes] = (mixed / totals[h, t]).astype(jnp.bfloat16)
-        ov[j] = jnp.dot(perm_t[...], op[...], preferred_element_type=jnp.float32).astype(
-            jnp.bfloat16
-        )
-        result(j).start()
+        o_ref[:, columns(j)] = jnp.dot(
+            perm_t[...], op[...], preferred_element_type=jnp.float32
+        ).astype(jnp.bfloat16)
 
     relay(0)
 
@@ -300,7 +294,6 @@
             def _():
                 detour(j, part).wait_send()
 
-        result(j).wait()
         return carry
 
     lax.fori_loop(0, chunks, finish, 0)
@@ -316,17 +309,16 @@
         tile = length // MOST
         span = (-(-WIN // tile) + 1) * tile
         half = jnp.bfloat16
-        anywhere = pl.BlockSpec(memory_space=pl.ANY)
+        hbm = pl.BlockSpec(memory_space=pltpu.HBM)
         scalars = pl.BlockSpec(memory_space=pltpu.SMEM)
         return pl.pallas_call(
             functools.partial(kernel, n, chunks),
-            out_shape=jax.ShapeDtypeStruct((length, width), half),
-            in_specs=[scalars, scalars, anywhere, anywhere, anywhere],
-            out_specs=anywhere,
+            out_shape=pltpu.VMEM((length, width), half),
+            in_specs=[scalars, scalars, hbm, hbm, hbm],
+            out_specs=pl.BlockSpec(memory_space=pltpu.VMEM),
             scratch_shapes=[
                 pltpu.VMEM((BACK, 2, chunks, length, cw), half),
                 pltpu.VMEM((3, chunks, length, cw), half),
-                pltpu.VMEM((chunks, length, cw), half),
                 pltpu.VMEM((length, length), half),
                 pltpu.VMEM((length, length), half),
                 pltpu.VMEM((2, (BACK + 1) * MOST, tile, cw), half),
@@ -337,9 +329,10 @@
                 pltpu.SemaphoreType.DMA((5, chunks, 2)),
                 pltpu.SemaphoreType.DMA((BACK, chunks, 2)),
                 pltpu.SemaphoreType.DMA((3, chunks)),
-                pltpu.SemaphoreType.DMA((chunks,)),
             ],
-            compiler_params=pltpu.CompilerParams(collective_id=0, has_side_effects=True),
+            compiler_params=pltpu.CompilerParams(
+                collective_id=0, has_side_effects=True, vmem_limit_bytes=60 * 2**20
+            ),
         )(dilation, window, queries, key_heads, value_heads)
 
     return jax.shard_map(

time: 58.2 us -> 56.3 us (0.967)
  local copies, waits for them, and re-layouts: 2.26 us -> 0.97 us
  Pallas kernels: 55.7 us -> 55.1 us
    unnamed x1, local copies, waits for them, and re-layouts: 2.26 us -> 0.97 us
    pallas_call x1, Pallas kernels: 55.7 us -> 55.1 us  [body(): pl.pallas_call(functools.partial(kernel, n, chunks), out_shape=pltpu.VMEM...]
where the time goes in v2:
time: 56.3 us; the launch traced here: 56.1 us
  Pallas kernels  55.1 us (98%)
  local copies, waits for them, and re-layouts  0.97 us (2%)
    pallas_call x1, Pallas kernels, body(): pl.pallas_call(functools.partial(kernel, n, chunks), out_shape=pltpu.VMEM...  55.1 us

profile of v2, /device:TPU:21, one launch (start us, length us, event | category | flops | bytes accessed | tf_op | source)
XLA Modules:
  0.0 56.1 jit_solution(4335806458656659510)
XLA Ops:
  0.0 55.1 %shard_map.55 = bf16[512,1024]{1,0:T(8,128)(2,1)S(1)} custom-call(s32[4]{0:T(128)} %dil_ref.1, s32[4]{0:T(128)} %win_ref.1, bf16[512,1024]{1,0:T(8,128)(2,1)} %q_ref.1, bf16[512,1024]{1,0:T(8,128)(2,1)} %k_ref.1, bf16[512,1024]{1,0:T(8,128)(2,1)} %v_ref.1), custom_call_target="tpu_custom_call" | custom-call | tf_op jit(solution)/shard_map/pallas_call | solution.py:314
  55.1 1.0 %copy.7 = bf16[512,1024]{1,0:T(8,128)(2,1)} copy(bf16[512,1024]{1,0:T(8,128)(2,1)S(1)} %shard_map.55) | data formatting | bytes 2097152

commit v3 on v2

--- a/solution.py
+++ b/solution.py
@@ -271,8 +271,8 @@
         def _():
             mix(j - 1)
 
+        fetch(j, 1)
         score(j)
-        fetch(j, 1)
         return carry
 
     lax.fori_loop(0, chunks, turn, 0)

time: 56.3 us -> 55 us (0.977)
  Pallas kernels: 55.1 us -> 53.5 us
    pallas_call x1, Pallas kernels: 55.1 us -> 53.5 us  [body(): pl.pallas_call(functools.partial(kernel, n, chunks), out_shape=pltpu.VMEM...]
where the time goes in v3:
time: 55 us; the launch traced here: 54.4 us
  Pallas kernels  53.5 us (97%)
  local copies, waits for them, and re-layouts  0.97 us (2%)
    pallas_call x1, Pallas kernels, body(): pl.pallas_call(functools.partial(kernel, n, chunks), out_shape=pltpu.VMEM...  53.5 us

profile of v3, /device:TPU:21, one launch (start us, length us, event | category | flops | bytes accessed | tf_op | source)
XLA Modules:
  0.0 54.4 jit_solution(852100189325386923)
XLA Ops:
  0.0 53.5 %shard_map.55 = bf16[512,1024]{1,0:T(8,128)(2,1)S(1)} custom-call(s32[4]{0:T(128)} %dil_ref.1, s32[4]{0:T(128)} %win_ref.1, bf16[512,1024]{1,0:T(8,128)(2,1)} %q_ref.1, bf16[512,1024]{1,0:T(8,128)(2,1)} %k_ref.1, bf16[512,1024]{1,0:T(8,128)(2,1)} %v_ref.1), custom_call_target="tpu_custom_call" | custom-call | tf_op jit(solution)/shard_map/pallas_call | solution.py:314
  53.5 1.0 %copy.7 = bf16[512,1024]{1,0:T(8,128)(2,1)} copy(bf16[512,1024]{1,0:T(8,128)(2,1)S(1)} %shard_map.55) | data formatting | bytes 2097152
